TPU v7x, 32 devices: a whole 2x2x4 slice. The times are simulated.
32 devices in a mesh: gx: 8 (over y, x, core), gy: 4 (over z).
Axes of the slice: x: 2, y: 2, z: 4, core: 2. Of those that a mesh axis runs over, the one named last changes fastest.
Arguments:
- volts: float32 [32, 4, 64, 512], P(None, None, 'gx', 'gy'), may hold values from -6 to 6
- cap: float32 [4, 64, 512], P(None, 'gx', 'gy'), may hold values from 0.05 to 1
- cond_x: float32 [4, 64, 512], P(None, 'gx', 'gy'), may hold values from 0.5 to 2
- cond_y: float32 [4, 64, 512], P(None, 'gx', 'gy'), may hold values from 0.5 to 2
- via: float32 [4, 64, 512], P(None, 'gx', 'gy'), may hold values from 0.2 to 2
- waveforms: float32 [64, 64], replicated, may hold values from -6 to 6
- placement: int32 [262144, 1], P(('gx', 'gy')), may hold values from 0 to 31; in each aligned block of 8192 rows (0 to 8191, 8192 to 16383, ...) at most 512 rows name the same one
- cells: int32 [262144], P(('gx', 'gy')), may hold values from 0 to 1023
- wave_ids: int32 [262144], P(('gx', 'gy')), may hold values from 0 to 63
- amps: float32 [262144], P(('gx', 'gy')), may hold values from 0.5 to 4
Outputs:
- volts_out: float32 [32, 4, 64, 512], P(None, None, 'gx', 'gy')
- residual: float32 [32, 4, 64, 512], P(None, None, 'gx', 'gy')
Inputs may be any that keep to these rules, and one draw needn't show every extreme that they name: `placement`: in each device's block of 8192 rows no tile is named more than 512 times, a bound that some block reaches.
All inputs are finite; a program needn't handle non-finite values.
Results may differ from a plain program's by a relative error of at most 0.0029.
Values may be sent and summed in bfloat16 or wider, within the bound.
A program may use at most 64 MiB of HBM per device.

v0:
```python
import jax
import jax.numpy as jnp
from jax import lax
from jax.sharding import PartitionSpec as P

ITERS = 3


def with_halo(block, sides, width):
    for axis, dim in sides:
        count = lax.axis_size(axis)
        forward = [(i, i + 1) for i in range(count - 1)]
        backward = [(target, source) for source, target in forward]
        low = lax.ppermute(
            lax.slice_in_dim(block, block.shape[dim] - width, None, axis=dim), axis, forward
        )
        high = lax.ppermute(lax.slice_in_dim(block, 0, width, axis=dim), axis, backward)
        block = jnp.concatenate([low, block, high], axis=dim)
    return block


def shifted(x, axis, by):
    length = lax.axis_size(axis)
    pairs = [(i, i + by) for i in range(length) if 0 <= i + by < length]
    return lax.ppermute(x, axis, pairs)


def gram(left, right):
    left_rows = left.reshape(left.shape[0], -1)
    right_rows = right.reshape(right.shape[0], -1)
    return lax.dot_general(
        left_rows, right_rows, (((1,), (1,)), ((), ())), precision=lax.Precision.HIGHEST
    )


def combine(coef, field):
    return jnp.einsum("st,slxy->tlxy", coef, field, precision=lax.Precision.HIGHEST)


def spd_solve(matrix, right):
    factor = jnp.linalg.cholesky(matrix)
    return jax.scipy.linalg.cho_solve((factor, True), right)


def make_currents(waveforms, kinds, scales):
    table_hits = (
        jnp.arange(waveforms.shape[1], dtype=jnp.int32)[:, None] == kinds[None, :]
    ).astype(jnp.float32)
    picked = jnp.dot(waveforms, table_hits, precision=lax.Precision.HIGHEST)
    return (picked * scales[None, :]).astype(jnp.bfloat16)


def operate(field, cap, cond_x, cond_x_low, cond_y, cond_y_low, via, via_low):
    padded = with_halo(field, (("gx", 2), ("gy", 3)), 1)
    zero_layer = jnp.zeros_like(field[:, :1])
    upper = jnp.concatenate([field[:, 1:], zero_layer], axis=1)
    lower = jnp.concatenate([zero_layer, field[:, :-1]], axis=1)
    result = cap * field
    result = result + cond_x * (field - padded[:, :, 2:, 1:-1])
    result = result + cond_x_low * (field - padded[:, :, :-2, 1:-1])
    result = result + cond_y * (field - padded[:, :, 1:-1, 2:])
    result = result + cond_y_low * (field - padded[:, :, 1:-1, :-2])
    result = result + via * (field - upper) + via_low * (field - lower)
    return result


def body(volts, cap, cond_x, cond_y, via, waveforms, placement, cells, wave_ids, amps):
    devices = lax.axis_size(("gx", "gy"))
    scenarios = volts.shape[0]
    steps = waveforms.shape[0] // scenarios
    tile_x = volts.shape[2]
    tile_y = volts.shape[3]
    die_cells = tile_x * tile_y
    slots_all = 2 * cells.shape[0]
    capacity = slots_all // devices
    target = placement[:, 0]
    target_hits = (jnp.arange(devices, dtype=jnp.int32)[:, None] == target[None, :]).astype(
        jnp.int32
    )
    running = jnp.cumsum(target_hits, axis=1) - 1
    position = jnp.sum(target_hits * running, axis=0)
    slot_index = target * capacity + position
    currents = make_currents(waveforms, wave_ids, amps)
    packed = jnp.zeros((currents.shape[0], slots_all), jnp.bfloat16).at[:, slot_index].set(currents)
    cell_slots = jnp.zeros((1, slots_all), jnp.int32).at[0, slot_index].set(cells)
    arrived, cell_slots = (
        lax.all_to_all(packed, ("gx", "gy"), split_axis=1, concat_axis=1, tiled=True),
        lax.all_to_all(cell_slots, ("gx", "gy"), split_axis=1, concat_axis=1, tiled=True),
    )
    block_rows = min(1024, slots_all)
    block_count = slots_all // block_rows
    cell_line = jnp.arange(die_cells, dtype=jnp.int32)

    def add_block(turn, total):
        piece_values = lax.dynamic_slice_in_dim(arrived, turn * block_rows, block_rows, 1)
        piece_cells = lax.dynamic_slice_in_dim(cell_slots[0], turn * block_rows, block_rows, 0)
        one_hot = (piece_cells[:, None] == cell_line[None, :]).astype(jnp.bfloat16)
        return total + jnp.dot(piece_values, one_hot, preferred_element_type=jnp.float32)

    injected = lax.fori_loop(
        0, block_count, add_block, jnp.zeros((arrived.shape[0], die_cells), jnp.float32)
    )
    injected = injected.reshape(steps, scenarios, tile_x, tile_y)
    rim_x = shifted(cond_x[:, -1:, :], "gx", 1)
    rim_y = shifted(cond_y[:, :, -1:], "gy", 1)
    cond_x_low = jnp.concatenate([rim_x, cond_x[:, :-1, :]], axis=1)
    cond_y_low = jnp.concatenate([rim_y, cond_y[:, :, :-1]], axis=2)
    via_low = jnp.concatenate([jnp.zeros_like(via[:1]), via[:-1]], axis=0)

    def apply_grid(field):
        return operate(field, cap, cond_x, cond_x_low, cond_y, cond_y_low, via, via_low)

    voltage = volts
    residual = volts
    for step in range(steps):
        rhs = cap * voltage
        rhs = rhs.at[:, 0].add(-injected[step])
        iterate = voltage
        residual = rhs - apply_grid(iterate)
        direction = residual
        norm_gram = lax.psum(gram(residual, residual), ("gx", "gy"))
        for sweep in range(ITERS):
            image = apply_grid(direction)
            curve_gram, cross_gram, image_gram = lax.psum(
                (gram(direction, image), gram(residual, image), gram(image, image)), ("gx", "gy")
            )
            step_coef = spd_solve(curve_gram, norm_gram)
            iterate = iterate + combine(step_coef, direction)
            residual = residual - combine(step_coef, image)
            if sweep + 1 < ITERS:
                cross_term = jnp.dot(cross_gram, step_coef, precision=lax.Precision.HIGHEST)
                square_term = jnp.dot(
                    step_coef.T,
                    jnp.dot(image_gram, step_coef, precision=lax.Precision.HIGHEST),
                    precision=lax.Precision.HIGHEST,
                )
                new_gram = norm_gram - cross_term - cross_term.T + square_term
                turn_coef = spd_solve(norm_gram, new_gram)
                direction = residual + combine(turn_coef, direction)
                norm_gram = new_gram
        voltage = iterate
    return (voltage, residual)


def solution(mesh):
    return jax.shard_map(
        body,
        mesh=mesh,
        in_specs=(
            P(None, None, "gx", "gy"),
            P(None, "gx", "gy"),
            P(None, "gx", "gy"),
            P(None, "gx", "gy"),
            P(None, "gx", "gy"),
            P(),
            P(("gx", "gy"), None),
            P(("gx", "gy")),
            P(("gx", "gy")),
            P(("gx", "gy")),
        ),
        out_specs=(P(None, None, "gx", "gy"), P(None, None, "gx", "gy")),
        check_vma=False,
    )
```

profile of v0, /device:TPU:0, one launch (start us, length us, event | category | flops | bytes accessed | tf_op | source)
XLA Modules:
  0.0 647.4 jit_solution(1546838298687216187)
XLA Ops:
  1.6 9.5 %reduce-window.6 = s32[32,64,128]{2,1,0:T(8,128)S(1)} reduce-window(s32[32,64,128]{2,1,0:T(8,128)S(1)} %fusion.11, s32[]{:T(128)} %constant.128.clone.1), window={size=1x1x128 pad=0_0x0_0x127_0}, to_apply=%region_0.0 | reduce-window | flops 33292288 | bytes 2097156 | tf_op jit(solution)/shard_map/reduce-window
  14.9 23.7 %scatter_custom_fusion = bf16[64,16384]{0,1:T(8,128)(2,1)} fusion(s32[8192]{0:T(1024)S(1)} %bitcast.343, bf16[8192,64]{1,0:T(8,128)(2,1)S(1)} %copy.219, bf16[]{:T(256)} %constant.130.clone.1), kind=kCustom, calls=%fused_computation.13 | custom fusion | bytes 2097154 | tf_op jit(solution)/shard_map/scatter | solution.py:84
  38.6 4.8 copy.220
  43.3 7.3 %all-to-all-start = ((bf16[64,32,512]{2,0,1:T(8,128)(2,1)}), bf16[64,32,512]{2,0,1:T(8,128)(2,1)S(1)}, u32[]{:S(2)}, u32[]{:S(2)}) async-start(bf16[64,32,512]{2,0,1:T(8,128)(2,1)} %copy.220), calls=%async_computation | async-start | bytes 4194304 | tf_op jit(solution)/shard_map/all_to_all | solution.py:87
  55.2 3.5 collective-permute-start.4
  58.8 3.7 collective-permute-start.1
  62.9 31.2 %scatter_custom_fusion.1 = s32[16384]{0:T(1024)} fusion(s32[8192]{0:T(1024)S(1)} %broadcast_select_fusion, s32[8192]{0:T(1024)} %param.26, s32[]{:T(128)} %constant.128.clone.1), kind=kCustom, calls=%fused_computation.270 | custom fusion | bytes 66048
  97.6 7.3 %all-to-all-start.1 = ((s32[1,32,512]{2,0,1:T(1,128)}), s32[1,32,512]{2,0,1:T(1,128)}, u32[]{:S(2)}, u32[]{:S(2)}) async-start(s32[1,32,512]{2,0,1:T(1,128)} %bitcast.344), calls=%async_computation.1 | async-start | bytes 131072 | tf_op jit(solution)/shard_map/all_to_all | solution.py:88
  110.3 4.7 collective-permute-start.5
  119.0 53.7 %while.16 = (s32[]{:T(128)}, f32[64,1024]{1,0:T(8,128)}, bf16[64,16384]{1,0:T(8,128)(2,1)}, s32[1,16384]{1,0:T(1,128)}, s32[]{:T(128)}, /*index=5*/s32[]{:T(128)}, s32[]{:T(128)}, s32[]{:T(128)}) while((s32[]{:T(128)}, f32[64,1024]{1,0:T(8,128)}, bf16[64,16384]{1,0:T(8,128)(2,1)}, s32[1,16384]{1,0:T(1,128)}, s32[]{:T(128)}, ...), condition=%wide.region_6.7_spmd.clone, body=%wide.region_5.6_spmd.clone.sunk | while | flops 135397376 | bytes 667797 | solution.py:100
  123.1 2.7 fusion.346
  136.5 2.7 fusion.346
  149.9 2.7 fusion.346
  153.3 2.7 fusion.346
  163.3 2.7 fusion.346
  166.7 2.7 fusion.346
  177.6 3.0 collective-permute-start.7
  183.8 4.8 collective-permute-start.9
  192.3 44.5 %all-reduce.21 = (f32[32,32]{0,1:T(8,128)S(1)}, f32[32,32]{0,1:T(8,128)S(1)}, f32[32,32]{1,0:T(8,128)S(1)}) all-reduce(f32[32,32]{0,1:T(8,128)S(1)} %convolution_bitcast_fusion.18, f32[32,32]{0,1:T(8,128)S(1)} %convolution_bitcast_fusion.19, f32[32,32]{1,0:T(8,128)S(1)} %convolution_bitcast_fusion.17), channel_id=1, replica_groups=mesh['gx'=8,'gy'=4] {'gx','gy'}, use_global_device_ids=true, to_apply=%region_10.12 | all-reduce | flops 3072 | bytes 24576 | tf_op jit(solution)/shard_map/psum | solution.py:121
  236.9 2.9 cholesky.164
  245.4 2.9 cholesky.175
  255.0 2.9 cholesky.197
  259.2 3.0 collective-permute-start.11
  266.5 4.8 collective-permute-start.13
  271.9 3.1 custom-call.20
  279.1 43.3 %all-reduce.20 = (f32[32,32]{0,1:T(8,128)S(1)}, f32[32,32]{1,0:T(8,128)S(1)}, f32[32,32]{1,0:T(8,128)S(1)}) all-reduce(f32[32,32]{0,1:T(8,128)S(1)} %convolution_bitcast_fusion.15, f32[32,32]{1,0:T(8,128)S(1)} %convolution_bitcast_fusion.13, f32[32,32]{1,0:T(8,128)S(1)} %convolution_bitcast_fusion.14), channel_id=1, replica_groups=mesh['gx'=8,'gy'=4] {'gx','gy'}, use_global_device_ids=true, to_apply=%region_12.15 | all-reduce | flops 3072 | bytes 24576 | tf_op jit(solution)/shard_map/psum | solution.py:124
  322.6 2.9 cholesky.186
  333.2 3.0 collective-permute-start.15
  340.4 4.5 collective-permute-start.17
  347.8 43.9 %psum.110 = f32[32,32]{0,1:T(8,128)S(1)} all-reduce(f32[32,32]{0,1:T(8,128)S(1)} %convolution_bitcast_fusion.11), channel_id=1, replica_groups=mesh['gx'=8,'gy'=4] {'gx','gy'}, use_global_device_ids=true, to_apply=%region_15.18 | all-reduce | flops 1024 | bytes 8192 | tf_op jit(solution)/shard_map/psum | solution.py:124
  391.7 2.9 cholesky.208
  400.8 3.0 collective-permute-start.19
  408.1 5.0 collective-permute-start.21
  417.5 3.3 collective-permute-start.23
  425.1 4.6 collective-permute-start.25
  434.3 46.8 %all-reduce.19 = (f32[32,32]{0,1:T(8,128)S(1)}, f32[32,32]{0,1:T(8,128)S(1)}, f32[32,32]{1,0:T(8,128)S(1)}) all-reduce(f32[32,32]{0,1:T(8,128)S(1)} %convolution_bitcast_fusion.8, f32[32,32]{0,1:T(8,128)S(1)} %convolution_bitcast_fusion.9, f32[32,32]{1,0:T(8,128)S(1)} %convolution_bitcast_fusion.7), channel_id=1, replica_groups=mesh['gx'=8,'gy'=4] {'gx','gy'}, use_global_device_ids=true, to_apply=%region_17.20 | all-reduce | flops 3072 | bytes 24576 | tf_op jit(solution)/shard_map/psum | solution.py:121
  481.2 2.9 cholesky.219
  489.7 2.9 cholesky.230
  499.9 2.9 cholesky.252
  504.1 3.0 collective-permute-start.27
  510.3 4.7 collective-permute-start.29
  515.7 3.1 custom-call.25
  522.7 42.7 %all-reduce.18 = (f32[32,32]{0,1:T(8,128)S(1)}, f32[32,32]{1,0:T(8,128)S(1)}, f32[32,32]{1,0:T(8,128)S(1)}) all-reduce(f32[32,32]{0,1:T(8,128)S(1)} %convolution_bitcast_fusion.5, f32[32,32]{1,0:T(8,128)S(1)} %convolution_bitcast_fusion.3, f32[32,32]{1,0:T(8,128)S(1)} %convolution_bitcast_fusion.4), channel_id=1, replica_groups=mesh['gx'=8,'gy'=4] {'gx','gy'}, use_global_device_ids=true, to_apply=%region_19.22 | all-reduce | flops 3072 | bytes 24576 | tf_op jit(solution)/shard_map/psum | solution.py:124
  565.5 2.9 cholesky.241
  576.2 3.0 collective-permute-start.31
  583.3 4.5 collective-permute-start.33
  592.0 44.5 %psum.117 = f32[32,32]{0,1:T(8,128)S(1)} all-reduce(f32[32,32]{0,1:T(8,128)S(1)} %convolution_bitcast_fusion.1), channel_id=1, replica_groups=mesh['gx'=8,'gy'=4] {'gx','gy'}, use_global_device_ids=true, to_apply=%region_22.25 | all-reduce | flops 1024 | bytes 8192 | tf_op jit(solution)/shard_map/psum | solution.py:124
  636.6 2.9 cholesky.263
  (373 shorter events, 177.7 us)
Async XLA Ops:
  43.3 15.4 %copy-start.11 = (f32[4,8,128]{2,1,0:T(8,128)S(1)}, f32[4,8,128]{2,1,0:T(8,128)}, u32[]{:S(2)}) copy-start(f32[4,8,128]{2,1,0:T(8,128)} %param.21) | copy-start | bytes 49156
  43.3 19.2 %copy-start.32 = (s32[2]{0:T(128)S(1)}, s32[2]{0:T(128)}, u32[]{:S(2)}) copy-start(s32[2]{0:T(128)} %constant.170) | copy-start | bytes 28
  43.3 19.3 %copy-start.33 = (s32[2]{0:T(128)S(1)}, s32[2]{0:T(128)}, u32[]{:S(2)}) copy-start(s32[2]{0:T(128)} %constant.173) | copy-start | bytes 28
  43.3 54.2 %all-to-all-start = ((bf16[64,32,512]{2,0,1:T(8,128)(2,1)}), bf16[64,32,512]{2,0,1:T(8,128)(2,1)S(1)}, u32[]{:S(2)}, u32[]{:S(2)}) async-start(bf16[64,32,512]{2,0,1:T(8,128)(2,1)} %copy.220), calls=%async_computation | async-start | bytes 4194304 | tf_op jit(solution)/shard_map/all_to_all | solution.py:87
  50.7 44.4 %slice-start = ((f32[4,8,128]{2,1,0:T(8,128)}), f32[3,8,128]{2,1,0:T(8,128)S(1)}, s32[]{:S(2)}) async-start(f32[4,8,128]{2,1,0:T(8,128)} %param.23), calls=%async_computation.2 | async-start | bytes 24576 | tf_op jit(solution)/shard_map/slice | solution.py:108
  50.7 44.5 %copy-start.9 = (f32[4,8,128]{2,1,0:T(8,128)S(1)}, f32[4,8,128]{2,1,0:T(8,128)}, u32[]{:S(2)}) copy-start(f32[4,8,128]{2,1,0:T(8,128)} %param.20) | copy-start | bytes 49156
  51.7 43.5 %collective-permute-start.2 = (f32[32,4,1,128]{3,0,2,1:T(8,128)S(1)}, f32[32,4,1,128]{3,0,2,1:T(8,128)S(1)}, u32[]{:S(2)}, u32[]{:S(2)}) collective-permute-start(f32[32,4,1,128]{3,0,2,1:T(8,128)S(1)} %get-tuple-element.215), channel_id=1, source_target_pairs={{0,4},{4,8},{8,12},{12,16},{16,20},{20,24},{24,28},{1,5},{5,9},{9,... | collective-permute-start | bytes 196616 | tf_op jit(solution)/shard_map/ppermute | solution.py:14
  53.8 43.6 %collective-permute-start = (f32[32,4,1,128]{3,0,2,1:T(8,128)}, f32[32,4,1,128]{3,0,2,1:T(8,128)S(1)}, u32[]{:S(2)}, u32[]{:S(2)}) collective-permute-start(f32[32,4,1,128]{3,0,2,1:T(8,128)} %get-tuple-element.214), channel_id=1, source_target_pairs={{4,0},{8,4},{12,8},{16,12},{20,16},{24,20},{28,24},{5,1},{9,5},{13... | collective-permute-start | bytes 196616 | tf_op jit(solution)/shard_map/ppermute | solution.py:17
  55.2 39.9 %collective-permute-start.4 = (f32[4,8,1]{2,1,0:T(8,128)S(1)}, f32[4,8,1]{2,1,0:T(8,128)S(1)}, u32[]{:S(2)}, u32[]{:S(2)}) collective-permute-start(f32[4,8,1]{2,1,0:T(8,128)S(1)} %slice.379), channel_id=1, source_target_pairs={{0,1},{1,2},{2,3},{4,5},{5,6},{6,7},{8,9},{9,10},{10,11},{12,13},{... | collective-permute-start | bytes 392 | tf_op jit(solution)/shard_map/ppermute | solution.py:25
  58.8 56.2 %collective-permute-start.1 = (f32[4,1,128]{2,1,0:T(1,128)S(1)}, f32[4,1,128]{2,1,0:T(1,128)S(1)}, u32[]{:S(2)}, u32[]{:S(2)}) collective-permute-start(f32[4,1,128]{2,1,0:T(1,128)S(1)} %slice.373), channel_id=1, source_target_pairs={{0,4},{4,8},{8,12},{12,16},{16,20},{20,24},{24,28},{1,5},{5,9},{9,... | collective-permute-start | bytes 6152 | tf_op jit(solution)/shard_map/ppermute | solution.py:25
  97.6 21.4 %all-to-all-start.1 = ((s32[1,32,512]{2,0,1:T(1,128)}), s32[1,32,512]{2,0,1:T(1,128)}, u32[]{:S(2)}, u32[]{:S(2)}) async-start(s32[1,32,512]{2,0,1:T(1,128)} %bitcast.344), calls=%async_computation.1 | async-start | bytes 131072 | tf_op jit(solution)/shard_map/all_to_all | solution.py:88
  107.6 7.4 %collective-permute-start.3 = (f32[32,4,10,1]{0,1,3,2:T(4,128)S(1)}, f32[32,4,10,1]{0,1,3,2:T(4,128)S(1)}, u32[]{:S(2)}, u32[]{:S(2)}) collective-permute-start(f32[32,4,10,1]{0,1,3,2:T(4,128)S(1)} %copy.230), channel_id=1, source_target_pairs={{1,0},{2,1},{3,2},{5,4},{6,5},{7,6},{9,8},{10,9},{11,10},{13,12},{... | collective-permute-start | bytes 15368 | tf_op jit(solution)/shard_map/ppermute | solution.py:17
  110.3 6.0 collective-permute-start.5
  119.0 55.4 %copy-start.4 = (f32[32,4,8,128]{3,0,2,1:T(8,128)S(1)}, f32[32,4,8,128]{3,0,2,1:T(8,128)}, u32[]{:S(2)}) copy-start(f32[32,4,8,128]{3,0,2,1:T(8,128)} %get-tuple-element.217) | copy-start | bytes 1572868
  119.0 55.5 %copy-start.5 = (f32[32,4,10,1]{3,0,2,1:T(8,128)S(1)}, f32[32,4,10,1]{3,0,2,1:T(8,128)}, u32[]{:S(2)}) copy-start(f32[32,4,10,1]{3,0,2,1:T(8,128)} %copy.231) | copy-start | bytes 15364
  119.0 55.5 %copy-start.7 = (f32[32,3,8,128]{3,0,2,1:T(8,128)S(1)}, f32[32,3,8,128]{3,0,2,1:T(8,128)}, u32[]{:S(2)}) copy-start(f32[32,3,8,128]{3,0,2,1:T(8,128)} %get-tuple-element.212) | copy-start | bytes 1179652
  119.0 55.5 %copy-start.12 = (f32[4,8,128]{2,1,0:T(8,128)S(1)}, f32[4,8,128]{2,1,0:T(8,128)}, u32[]{:S(2)}) copy-start(f32[4,8,128]{2,1,0:T(8,128)} %param.23) | copy-start | bytes 49156
  176.3 4.4 collective-permute-start.6
  177.6 3.9 collective-permute-start.7
  182.2 7.7 %collective-permute-start.8 = (f32[32,4,10,1]{0,1,3,2:T(4,128)S(1)}, f32[32,4,10,1]{0,1,3,2:T(4,128)S(1)}, u32[]{:S(2)}, u32[]{:S(2)}) collective-permute-start(f32[32,4,10,1]{0,1,3,2:T(4,128)S(1)} %copy.240), channel_id=1, source_target_pairs={{1,0},{2,1},{3,2},{5,4},{6,5},{7,6},{9,8},{10,9},{11,10},{13,12},{... | collective-permute-start | bytes 15368 | tf_op jit(solution)/shard_map/ppermute | solution.py:17
  183.8 6.4 collective-permute-start.9
  257.9 5.1 collective-permute-start.10
  259.2 3.9 collective-permute-start.11
  264.9 10.1 %collective-permute-start.12 = (f32[32,4,10,1]{0,1,3,2:T(4,128)S(1)}, f32[32,4,10,1]{0,1,3,2:T(4,128)S(1)}, u32[]{:S(2)}, u32[]{:S(2)}) collective-permute-start(f32[32,4,10,1]{0,1,3,2:T(4,128)S(1)} %copy.254), channel_id=1, source_target_pairs={{1,0},{2,1},{3,2},{5,4},{6,5},{7,6},{9,8},{10,9},{11,10},{13,12},{... | collective-permute-start | bytes 15368 | tf_op jit(solution)/shard_map/ppermute | solution.py:17
  266.5 8.9 %collective-permute-start.13 = (f32[32,4,10,1]{0,1,3,2:T(4,128)S(1)}, f32[32,4,10,1]{0,1,3,2:T(4,128)S(1)}, u32[]{:S(2)}, u32[]{:S(2)}) collective-permute-start(f32[32,4,10,1]{0,1,3,2:T(4,128)S(1)} %copy.256), channel_id=1, source_target_pairs={{0,1},{1,2},{2,3},{4,5},{5,6},{6,7},{8,9},{9,10},{10,11},{12,13},{... | collective-permute-start | bytes 15368 | tf_op jit(solution)/shard_map/ppermute | solution.py:14
  278.0 52.9 %copy-start.30 = (f32[1,32,32]{1,2,0:T(8,128)S(1)}, f32[1,32,32]{1,2,0:T(8,128)}, u32[]{:S(2)}) copy-start(f32[1,32,32]{1,2,0:T(8,128)} %custom-call.20) | copy-start | bytes 12292
  331.9 5.0 collective-permute-start.14
  333.2 3.9 collective-permute-start.15
  338.8 6.3 collective-permute-start.16
  340.4 6.0 collective-permute-start.17
  399.5 5.2 collective-permute-start.18
  400.8 3.9 collective-permute-start.19
  406.5 6.6 %collective-permute-start.20 = (f32[32,4,10,1]{0,1,3,2:T(4,128)S(1)}, f32[32,4,10,1]{0,1,3,2:T(4,128)S(1)}, u32[]{:S(2)}, u32[]{:S(2)}) collective-permute-start(f32[32,4,10,1]{0,1,3,2:T(4,128)S(1)} %copy.274), channel_id=1, source_target_pairs={{1,0},{2,1},{3,2},{5,4},{6,5},{7,6},{9,8},{10,9},{11,10},{13,12},{... | collective-permute-start | bytes 15368 | tf_op jit(solution)/shard_map/ppermute | solution.py:17
  408.1 6.0 collective-permute-start.21
  416.2 5.4 collective-permute-start.22
  417.5 4.2 collective-permute-start.23
  423.5 6.7 %collective-permute-start.24 = (f32[32,4,10,1]{0,1,3,2:T(4,128)S(1)}, f32[32,4,10,1]{0,1,3,2:T(4,128)S(1)}, u32[]{:S(2)}, u32[]{:S(2)}) collective-permute-start(f32[32,4,10,1]{0,1,3,2:T(4,128)S(1)} %copy.278), channel_id=1, source_target_pairs={{1,0},{2,1},{3,2},{5,4},{6,5},{7,6},{9,8},{10,9},{11,10},{13,12},{... | collective-permute-start | bytes 15368 | tf_op jit(solution)/shard_map/ppermute | solution.py:17
  425.1 6.0 collective-permute-start.25
  502.8 5.0 collective-permute-start.26
  504.1 3.9 collective-permute-start.27
  508.7 10.0 %collective-permute-start.28 = (f32[32,4,10,1]{0,1,3,2:T(4,128)S(1)}, f32[32,4,10,1]{0,1,3,2:T(4,128)S(1)}, u32[]{:S(2)}, u32[]{:S(2)}) collective-permute-start(f32[32,4,10,1]{0,1,3,2:T(4,128)S(1)} %copy.291), channel_id=1, source_target_pairs={{1,0},{2,1},{3,2},{5,4},{6,5},{7,6},{9,8},{10,9},{11,10},{13,12},{... | collective-permute-start | bytes 15368 | tf_op jit(solution)/shard_map/ppermute | solution.py:17
  510.3 8.8 %collective-permute-start.29 = (f32[32,4,10,1]{0,1,3,2:T(4,128)S(1)}, f32[32,4,10,1]{0,1,3,2:T(4,128)S(1)}, u32[]{:S(2)}, u32[]{:S(2)}) collective-permute-start(f32[32,4,10,1]{0,1,3,2:T(4,128)S(1)} %copy.293), channel_id=1, source_target_pairs={{0,1},{1,2},{2,3},{4,5},{5,6},{6,7},{8,9},{9,10},{10,11},{12,13},{... | collective-permute-start | bytes 15368 | tf_op jit(solution)/shard_map/ppermute | solution.py:14
  521.5 52.3 %copy-start.31 = (f32[1,32,32]{1,2,0:T(8,128)S(1)}, f32[1,32,32]{1,2,0:T(8,128)}, u32[]{:S(2)}) copy-start(f32[1,32,32]{1,2,0:T(8,128)} %custom-call.25) | copy-start | bytes 12292
  522.7 56.5 %copy-start.6 = (f32[32,4,8,128]{3,0,2,1:T(8,128)S(1)}, f32[32,4,8,128]{3,0,2,1:T(8,128)}, u32[]{:S(2)}) copy-start(f32[32,4,8,128]{3,0,2,1:T(8,128)} %convolution_add_fusion.4) | copy-start | bytes 1572868
  574.9 5.0 collective-permute-start.30
  576.2 3.9 collective-permute-start.31
  581.7 7.1 %collective-permute-start.32 = (f32[32,4,10,1]{0,1,3,2:T(4,128)S(1)}, f32[32,4,10,1]{0,1,3,2:T(4,128)S(1)}, u32[]{:S(2)}, u32[]{:S(2)}) collective-permute-start(f32[32,4,10,1]{0,1,3,2:T(4,128)S(1)} %copy.303), channel_id=1, source_target_pairs={{1,0},{2,1},{3,2},{5,4},{6,5},{7,6},{9,8},{10,9},{11,10},{13,12},{... | collective-permute-start | bytes 15368 | tf_op jit(solution)/shard_map/ppermute | solution.py:17
  583.3 6.0 collective-permute-start.33
  (25 other events, 150.4 us)
where the time goes:
time: 657 us; the launch traced here: 647 us
  blocking collectives  266 us (40%)
  local copies, waits for them, and re-layouts  107 us (16%)
  starting transfers between devices  104 us (16%)
  other arithmetic  95.1 us (14%)
  matrix products  68.5 us (10%)
    psum x4, blocking collectives, body(): lax.psum((gram(direction, image), gram(residual, image), gram(image, imag...  174 us
    psum x2, blocking collectives, body(): norm_gram = lax.psum(gram(residual, residual), ('gx', 'gy'))  91.3 us
    ppermute x16, starting transfers between devices, with_halo(): lax.ppermute(lax.slice_in_dim(block, block.shape[dim] - width, None, axis...  61.3 us
    dot_general x16, matrix products, add_block(): jnp.dot(piece_values, one_hot, preferred_element_type=jnp.float32)  42.7 us
    unnamed x79, local copies, waits for them, and re-layouts  40.2 us
    another operation x30, other arithmetic, spd_solve(): factor = jnp.linalg.cholesky(matrix)  36.1 us
    another operation x20, other arithmetic, spd_solve(): return jax.scipy.linalg.cho_solve((factor, True), right)  32.2 us
    scatter x1, local copies, waits for them, and re-layouts, body(): jnp.zeros((currents.shape[0], slots_all), jnp.bfloat16).at[:, slot_index]  23.7 us
  transfers between devices with their start and end apart: 36, of which 11 were waited for; matrix products, arithmetic and copies ran while one was open for 10% of the time, Pallas kernels for 0%

commit v1 on v0

--- a/solution.py
+++ b/solution.py
@@ -118,7 +118,7 @@
         iterate = voltage
         residual = rhs - apply_grid(iterate)
         direction = residual
-        norm_gram = lax.psum(gram(residual, residual), ("gx", "gy"))
+        norm_gram = jnp.sum(lax.all_gather(gram(residual, residual), ("gx", "gy")), axis=0)
         for sweep in range(ITERS):
             image = apply_grid(direction)
             curve_gram, cross_gram, image_gram = lax.psum(

time: 657 us -> 790 us (1.20)
  blocking collectives: 266 us -> 400 us
    all_gather x0 -> x2, blocking collectives: none -> 145 us  [body(): lax.all_gather(gram(residual, residual), ('gx', 'gy'))]
    psum x2 -> x0, blocking collectives: 91.3 us -> none  [body(): norm_gram = lax.psum(gram(residual, residual), ('gx', 'gy'))]
    psum x4 -> x6, blocking collectives: 174 us -> 254 us  [body(): lax.psum((gram(direction, image), gram(residual, image), gram(image, imag...]
    unnamed x79 -> x81, local copies, waits for them, and re-layouts: 40.2 us -> 38.9 us
  transfers between devices with their start and end apart: 36 -> 36, of which waited for: 11 -> 9; matrix products, arithmetic and copies ran while one was open for 10% -> 10% of each run, Pallas kernels for 0% -> 0%
where the time goes in v1:
time: 790 us; the launch traced here: 780 us
  blocking collectives  400 us (51%)
  local copies, waits for them, and re-layouts  106 us (13%)
  starting transfers between devices  104 us (13%)
  other arithmetic  96.5 us (12%)
  matrix products  68.6 us (9%)
    psum x6, blocking collectives, body(): lax.psum((gram(direction, image), gram(residual, image), gram(image, imag...  254 us
    all_gather x2, blocking collectives, body(): lax.all_gather(gram(residual, residual), ('gx', 'gy'))  145 us
    ppermute x16, starting transfers between devices, with_halo(): lax.ppermute(lax.slice_in_dim(block, block.shape[dim] - width, None, axis...  61 us
    dot_general x16, matrix products, add_block(): jnp.dot(piece_values, one_hot, preferred_element_type=jnp.float32)  42.9 us
    unnamed x81, local copies, waits for them, and re-layouts  38.9 us
    another operation x30, other arithmetic, spd_solve(): factor = jnp.linalg.cholesky(matrix)  36 us
    another operation x20, other arithmetic, spd_solve(): return jax.scipy.linalg.cho_solve((factor, True), right)  33.3 us
    scatter x1, local copies, waits for them, and re-layouts, body(): jnp.zeros((currents.shape[0], slots_all), jnp.bfloat16).at[:, slot_index]  23.7 us
  transfers between devices with their start and end apart: 36, of which 9 were waited for; matrix products, arithmetic and copies ran while one was open for 10% of the time, Pallas kernels for 0%

profile of v1, /device:TPU:0, one launch (start us, length us, event | category | flops | bytes accessed | tf_op | source)
XLA Modules:
  0.0 779.8 jit_solution(13002598303979023152)
XLA Ops:
  1.6 9.5 %reduce-window.6 = s32[32,64,128]{2,1,0:T(8,128)S(1)} reduce-window(s32[32,64,128]{2,1,0:T(8,128)S(1)} %fusion.11, s32[]{:T(128)} %constant.129.clone.1), window={size=1x1x128 pad=0_0x0_0x127_0}, to_apply=%region_0.0 | reduce-window | flops 33292288 | bytes 2097156 | tf_op jit(solution)/shard_map/reduce-window
  14.9 23.7 %scatter_custom_fusion = bf16[64,16384]{0,1:T(8,128)(2,1)} fusion(s32[8192]{0:T(1024)S(1)} %bitcast.351, bf16[8192,64]{1,0:T(8,128)(2,1)S(1)} %copy.215, bf16[]{:T(256)} %constant.131.clone.1), kind=kCustom, calls=%fused_computation.13 | custom fusion | bytes 2097154 | tf_op jit(solution)/shard_map/scatter | solution.py:84
  38.5 4.8 copy.216
  43.3 7.3 all-to-all-start
  55.2 3.5 collective-permute-start.4
  58.8 3.7 collective-permute-start.1
  62.9 31.2 %scatter_custom_fusion.1 = s32[16384]{0:T(1024)} fusion(s32[8192]{0:T(1024)S(1)} %broadcast_select_fusion, s32[8192]{0:T(1024)} %param.26, s32[]{:T(128)} %constant.129.clone.1), kind=kCustom, calls=%fused_computation.270 | custom fusion | bytes 66048
  97.6 7.3 all-to-all-start.1
  110.2 4.7 collective-permute-start.5
  119.0 53.9 %while.16 = (s32[]{:T(128)}, f32[64,1024]{1,0:T(8,128)}, bf16[64,16384]{1,0:T(8,128)(2,1)}, s32[1,16384]{1,0:T(1,128)}, s32[]{:T(128)}, /*index=5*/s32[]{:T(128)}, s32[]{:T(128)}, s32[]{:T(128)}) while((s32[]{:T(128)}, f32[64,1024]{1,0:T(8,128)}, bf16[64,16384]{1,0:T(8,128)(2,1)}, s32[1,16384]{1,0:T(1,128)}, s32[]{:T(128)}, ...), condition=%wide.region_6.7_spmd.clone, body=%wide.region_5.6_spmd.clone.sunk | while | flops 135397376 | bytes 667797 | solution.py:100
  153.3 2.7 fusion.346
  163.4 2.7 fusion.346
  178.4 3.0 collective-permute-start.7
  181.4 72.7 %all-gather = f32[1024,32]{1,0:T(8,128)S(1)} all-gather(f32[32,32]{1,0:T(8,128)S(1)} %convolution_bitcast_fusion.18), channel_id=2, replica_groups=mesh['gx'=8,'gy'=4] {'gx','gy'}, dimensions={0}, use_global_device_ids=true | all-gather | bytes 135168 | tf_op jit(solution)/shard_map/all_gather | solution.py:121
  254.3 2.9 cholesky.175
  260.1 4.5 collective-permute-start.9
  265.3 3.1 custom-call.18
  271.5 38.5 %all-reduce.21 = (f32[32,32]{0,1:T(8,128)S(1)}, f32[32,32]{1,0:T(8,128)S(1)}) all-reduce(f32[32,32]{0,1:T(8,128)S(1)} %convolution_bitcast_fusion.19, f32[32,32]{1,0:T(8,128)S(1)} %convolution_bitcast_fusion.17), channel_id=1, replica_groups=mesh['gx'=8,'gy'=4] {'gx','gy'}, use_global_device_ids=true, to_apply=%region_7.8 | all-reduce | flops 2048 | bytes 16384 | tf_op jit(solution)/shard_map/psum | solution.py:124
  310.1 2.9 cholesky.164
  321.5 2.9 cholesky.197
  325.7 3.0 collective-permute-start.11
  332.9 4.8 collective-permute-start.13
  338.4 3.1 custom-call.20
  345.6 44.2 %all-reduce.20 = (f32[32,32]{0,1:T(8,128)S(1)}, f32[32,32]{1,0:T(8,128)S(1)}, f32[32,32]{1,0:T(8,128)S(1)}) all-reduce(f32[32,32]{0,1:T(8,128)S(1)} %convolution_bitcast_fusion.15, f32[32,32]{1,0:T(8,128)S(1)} %convolution_bitcast_fusion.13, f32[32,32]{1,0:T(8,128)S(1)} %convolution_bitcast_fusion.14), channel_id=1, replica_groups=mesh['gx'=8,'gy'=4] {'gx','gy'}, use_global_device_ids=true, to_apply=%region_12.15 | all-reduce | flops 3072 | bytes 24576 | tf_op jit(solution)/shard_map/psum | solution.py:124
  389.9 2.9 cholesky.186
  400.6 3.0 collective-permute-start.15
  407.8 4.5 collective-permute-start.17
  415.1 43.8 %psum.95 = f32[32,32]{0,1:T(8,128)S(1)} all-reduce(f32[32,32]{0,1:T(8,128)S(1)} %convolution_bitcast_fusion.11), channel_id=1, replica_groups=mesh['gx'=8,'gy'=4] {'gx','gy'}, use_global_device_ids=true, to_apply=%region_15.18 | all-reduce | flops 1024 | bytes 8192 | tf_op jit(solution)/shard_map/psum | solution.py:124
  459.0 2.9 cholesky.208
  468.0 3.0 collective-permute-start.19
  475.4 5.0 collective-permute-start.21
  486.2 3.3 collective-permute-start.23
  489.5 72.6 %all-gather.1 = f32[1024,32]{1,0:T(8,128)S(1)} all-gather(f32[32,32]{1,0:T(8,128)S(1)} %convolution_bitcast_fusion.8), channel_id=3, replica_groups=mesh['gx'=8,'gy'=4] {'gx','gy'}, dimensions={0}, use_global_device_ids=true | all-gather | bytes 135168 | tf_op jit(solution)/shard_map/all_gather | solution.py:121
  562.2 2.9 cholesky.230
  568.0 4.5 collective-permute-start.25
  573.2 3.1 custom-call.23
  579.7 39.3 %all-reduce.19 = (f32[32,32]{0,1:T(8,128)S(1)}, f32[32,32]{1,0:T(8,128)S(1)}) all-reduce(f32[32,32]{0,1:T(8,128)S(1)} %convolution_bitcast_fusion.9, f32[32,32]{1,0:T(8,128)S(1)} %convolution_bitcast_fusion.7), channel_id=1, replica_groups=mesh['gx'=8,'gy'=4] {'gx','gy'}, use_global_device_ids=true, to_apply=%region_16.19 | all-reduce | flops 2048 | bytes 16384 | tf_op jit(solution)/shard_map/psum | solution.py:124
  619.1 2.9 cholesky.219
  631.0 2.9 cholesky.252
  635.3 3.0 collective-permute-start.27
  642.4 4.7 collective-permute-start.29
  647.7 3.1 custom-call.25
  654.9 44.3 %all-reduce.18 = (f32[32,32]{0,1:T(8,128)S(1)}, f32[32,32]{1,0:T(8,128)S(1)}, f32[32,32]{1,0:T(8,128)S(1)}) all-reduce(f32[32,32]{0,1:T(8,128)S(1)} %convolution_bitcast_fusion.5, f32[32,32]{1,0:T(8,128)S(1)} %convolution_bitcast_fusion.3, f32[32,32]{1,0:T(8,128)S(1)} %convolution_bitcast_fusion.4), channel_id=1, replica_groups=mesh['gx'=8,'gy'=4] {'gx','gy'}, use_global_device_ids=true, to_apply=%region_19.22 | all-reduce | flops 3072 | bytes 24576 | tf_op jit(solution)/shard_map/psum | solution.py:124
  699.3 2.9 cholesky.241
  709.9 3.0 collective-permute-start.31
  716.1 4.5 collective-permute-start.33
  724.8 44.2 %psum.101 = f32[32,32]{0,1:T(8,128)S(1)} all-reduce(f32[32,32]{0,1:T(8,128)S(1)} %convolution_bitcast_fusion.1), channel_id=1, replica_groups=mesh['gx'=8,'gy'=4] {'gx','gy'}, use_global_device_ids=true, to_apply=%region_22.25 | all-reduce | flops 1024 | bytes 8192 | tf_op jit(solution)/shard_map/psum | solution.py:124
  769.0 2.9 cholesky.263
  (380 shorter events, 181.1 us)
Async XLA Ops:
  43.3 19.3 %copy-start.34 = (s32[2]{0:T(128)S(1)}, s32[2]{0:T(128)}, u32[]{:S(2)}) copy-start(s32[2]{0:T(128)} %constant.174) | copy-start | bytes 28
  43.3 54.2 %all-to-all-start = ((bf16[64,32,512]{2,0,1:T(8,128)(2,1)}), bf16[64,32,512]{2,0,1:T(8,128)(2,1)S(1)}, u32[]{:S(2)}, u32[]{:S(2)}) async-start(bf16[64,32,512]{2,0,1:T(8,128)(2,1)} %copy.216), calls=%async_computation | async-start | bytes 4194304 | tf_op jit(solution)/shard_map/all_to_all | solution.py:87
  50.7 44.4 %slice-start = ((f32[4,8,128]{2,1,0:T(8,128)}), f32[3,8,128]{2,1,0:T(8,128)S(1)}, s32[]{:S(2)}) async-start(f32[4,8,128]{2,1,0:T(8,128)} %param.23), calls=%async_computation.2 | async-start | bytes 24576 | tf_op jit(solution)/shard_map/slice | solution.py:108
  50.7 44.5 %copy-start.8 = (f32[4,8,128]{2,1,0:T(8,128)S(1)}, f32[4,8,128]{2,1,0:T(8,128)}, u32[]{:S(2)}) copy-start(f32[4,8,128]{2,1,0:T(8,128)} %param.20) | copy-start | bytes 49156
  51.7 43.5 %collective-permute-start.2 = (f32[32,4,1,128]{3,0,2,1:T(8,128)S(1)}, f32[32,4,1,128]{3,0,2,1:T(8,128)S(1)}, u32[]{:S(2)}, u32[]{:S(2)}) collective-permute-start(f32[32,4,1,128]{3,0,2,1:T(8,128)S(1)} %get-tuple-element.213), channel_id=1, source_target_pairs={{0,4},{4,8},{8,12},{12,16},{16,20},{20,24},{24,28},{1,5},{5,9},{9,... | collective-permute-start | bytes 196616 | tf_op jit(solution)/shard_map/ppermute | solution.py:14
  53.8 43.6 %collective-permute-start = (f32[32,4,1,128]{3,0,2,1:T(8,128)}, f32[32,4,1,128]{3,0,2,1:T(8,128)S(1)}, u32[]{:S(2)}, u32[]{:S(2)}) collective-permute-start(f32[32,4,1,128]{3,0,2,1:T(8,128)} %get-tuple-element.212), channel_id=1, source_target_pairs={{4,0},{8,4},{12,8},{16,12},{20,16},{24,20},{28,24},{5,1},{9,5},{13... | collective-permute-start | bytes 196616 | tf_op jit(solution)/shard_map/ppermute | solution.py:17
  55.2 39.9 %collective-permute-start.4 = (f32[4,8,1]{2,1,0:T(8,128)S(1)}, f32[4,8,1]{2,1,0:T(8,128)S(1)}, u32[]{:S(2)}, u32[]{:S(2)}) collective-permute-start(f32[4,8,1]{2,1,0:T(8,128)S(1)} %slice.379), channel_id=1, source_target_pairs={{0,1},{1,2},{2,3},{4,5},{5,6},{6,7},{8,9},{9,10},{10,11},{12,13},{... | collective-permute-start | bytes 392 | tf_op jit(solution)/shard_map/ppermute | solution.py:25
  58.8 56.2 %collective-permute-start.1 = (f32[4,1,128]{2,1,0:T(1,128)S(1)}, f32[4,1,128]{2,1,0:T(1,128)S(1)}, u32[]{:S(2)}, u32[]{:S(2)}) collective-permute-start(f32[4,1,128]{2,1,0:T(1,128)S(1)} %slice.373), channel_id=1, source_target_pairs={{0,4},{4,8},{8,12},{12,16},{16,20},{20,24},{24,28},{1,5},{5,9},{9,... | collective-permute-start | bytes 6152 | tf_op jit(solution)/shard_map/ppermute | solution.py:25
  97.6 21.4 %all-to-all-start.1 = ((s32[1,32,512]{2,0,1:T(1,128)}), s32[1,32,512]{2,0,1:T(1,128)}, u32[]{:S(2)}, u32[]{:S(2)}) async-start(s32[1,32,512]{2,0,1:T(1,128)} %bitcast.352), calls=%async_computation.1 | async-start | bytes 131072 | tf_op jit(solution)/shard_map/all_to_all | solution.py:88
  107.5 7.4 collective-permute-start.3
  110.2 6.0 collective-permute-start.5
  118.9 55.5 %copy-start.4 = (f32[32,4,8,128]{3,0,2,1:T(8,128)S(1)}, f32[32,4,8,128]{3,0,2,1:T(8,128)}, u32[]{:S(2)}) copy-start(f32[32,4,8,128]{3,0,2,1:T(8,128)} %get-tuple-element.215) | copy-start | bytes 1572868
  118.9 55.6 %copy-start.5 = (f32[32,4,10,1]{3,0,2,1:T(8,128)S(1)}, f32[32,4,10,1]{3,0,2,1:T(8,128)}, u32[]{:S(2)}) copy-start(f32[32,4,10,1]{3,0,2,1:T(8,128)} %copy.227) | copy-start | bytes 15364
  118.9 55.6 %copy-start.7 = (f32[32,3,8,128]{3,0,2,1:T(8,128)S(1)}, f32[32,3,8,128]{3,0,2,1:T(8,128)}, u32[]{:S(2)}) copy-start(f32[32,3,8,128]{3,0,2,1:T(8,128)} %get-tuple-element.210) | copy-start | bytes 1179652
  119.0 55.6 %copy-start.11 = (f32[4,8,128]{2,1,0:T(8,128)S(1)}, f32[4,8,128]{2,1,0:T(8,128)}, u32[]{:S(2)}) copy-start(f32[4,8,128]{2,1,0:T(8,128)} %param.23) | copy-start | bytes 49156
  177.1 80.8 %collective-permute-start.6 = (f32[32,4,1,128]{3,0,2,1:T(8,128)S(1)}, f32[32,4,1,128]{3,0,2,1:T(8,128)S(1)}, u32[]{:S(2)}, u32[]{:S(2)}) collective-permute-start(f32[32,4,1,128]{3,0,2,1:T(8,128)S(1)} %get-tuple-element.209), channel_id=1, source_target_pairs={{4,0},{8,4},{12,8},{16,12},{20,16},{24,20},{28,24},{5,1},{9,5},{13... | collective-permute-start | bytes 196616 | tf_op jit(solution)/shard_map/ppermute | solution.py:17
  178.4 79.5 %collective-permute-start.7 = (f32[32,4,1,128]{3,0,2,1:T(8,128)S(1)}, f32[32,4,1,128]{3,0,2,1:T(8,128)S(1)}, u32[]{:S(2)}, u32[]{:S(2)}) collective-permute-start(f32[32,4,1,128]{3,0,2,1:T(8,128)S(1)} %get-tuple-element.208), channel_id=1, source_target_pairs={{0,4},{4,8},{8,12},{12,16},{16,20},{20,24},{24,28},{1,5},{5,9},{9,... | collective-permute-start | bytes 196616 | tf_op jit(solution)/shard_map/ppermute | solution.py:14
  258.5 10.6 %collective-permute-start.8 = (f32[32,4,10,1]{0,1,3,2:T(4,128)S(1)}, f32[32,4,10,1]{0,1,3,2:T(4,128)S(1)}, u32[]{:S(2)}, u32[]{:S(2)}) collective-permute-start(f32[32,4,10,1]{0,1,3,2:T(4,128)S(1)} %copy.236), channel_id=1, source_target_pairs={{1,0},{2,1},{3,2},{5,4},{6,5},{7,6},{9,8},{10,9},{11,10},{13,12},{... | collective-permute-start | bytes 15368 | tf_op jit(solution)/shard_map/ppermute | solution.py:17
  260.1 9.3 %collective-permute-start.9 = (f32[32,4,10,1]{0,1,3,2:T(4,128)S(1)}, f32[32,4,10,1]{0,1,3,2:T(4,128)S(1)}, u32[]{:S(2)}, u32[]{:S(2)}) collective-permute-start(f32[32,4,10,1]{0,1,3,2:T(4,128)S(1)} %copy.238), channel_id=1, source_target_pairs={{0,1},{1,2},{2,3},{4,5},{5,6},{6,7},{8,9},{9,10},{10,11},{12,13},{... | collective-permute-start | bytes 15368 | tf_op jit(solution)/shard_map/ppermute | solution.py:14
  270.4 48.2 %copy-start.29 = (f32[1,32,32]{1,2,0:T(8,128)S(1)}, f32[1,32,32]{1,2,0:T(8,128)}, u32[]{:S(2)}) copy-start(f32[1,32,32]{1,2,0:T(8,128)} %custom-call.18) | copy-start | bytes 12292
  324.4 5.1 collective-permute-start.10
  325.7 3.9 collective-permute-start.11
  331.3 10.1 %collective-permute-start.12 = (f32[32,4,10,1]{0,1,3,2:T(4,128)S(1)}, f32[32,4,10,1]{0,1,3,2:T(4,128)S(1)}, u32[]{:S(2)}, u32[]{:S(2)}) collective-permute-start(f32[32,4,10,1]{0,1,3,2:T(4,128)S(1)} %copy.250), channel_id=1, source_target_pairs={{1,0},{2,1},{3,2},{5,4},{6,5},{7,6},{9,8},{10,9},{11,10},{13,12},{... | collective-permute-start | bytes 15368 | tf_op jit(solution)/shard_map/ppermute | solution.py:17
  332.9 8.9 %collective-permute-start.13 = (f32[32,4,10,1]{0,1,3,2:T(4,128)S(1)}, f32[32,4,10,1]{0,1,3,2:T(4,128)S(1)}, u32[]{:S(2)}, u32[]{:S(2)}) collective-permute-start(f32[32,4,10,1]{0,1,3,2:T(4,128)S(1)} %copy.252), channel_id=1, source_target_pairs={{0,1},{1,2},{2,3},{4,5},{5,6},{6,7},{8,9},{9,10},{10,11},{12,13},{... | collective-permute-start | bytes 15368 | tf_op jit(solution)/shard_map/ppermute | solution.py:14
  344.5 53.8 %copy-start.30 = (f32[1,32,32]{1,2,0:T(8,128)S(1)}, f32[1,32,32]{1,2,0:T(8,128)}, u32[]{:S(2)}) copy-start(f32[1,32,32]{1,2,0:T(8,128)} %custom-call.20) | copy-start | bytes 12292
  399.3 5.0 collective-permute-start.14
  400.6 3.9 collective-permute-start.15
  406.2 6.3 collective-permute-start.16
  407.8 6.0 collective-permute-start.17
  466.7 5.2 collective-permute-start.18
  468.0 3.9 collective-permute-start.19
  473.8 6.6 collective-permute-start.20
  475.4 6.0 collective-permute-start.21
  484.9 80.9 %collective-permute-start.22 = (f32[32,4,1,128]{3,0,2,1:T(8,128)S(1)}, f32[32,4,1,128]{3,0,2,1:T(8,128)S(1)}, u32[]{:S(2)}, u32[]{:S(2)}) collective-permute-start(f32[32,4,1,128]{3,0,2,1:T(8,128)S(1)} %get-tuple-element.193), channel_id=1, source_target_pairs={{4,0},{8,4},{12,8},{16,12},{20,16},{24,20},{28,24},{5,1},{9,5},{13... | collective-permute-start | bytes 196616 | tf_op jit(solution)/shard_map/ppermute | solution.py:17
  486.2 79.6 %collective-permute-start.23 = (f32[32,4,1,128]{3,0,2,1:T(8,128)S(1)}, f32[32,4,1,128]{3,0,2,1:T(8,128)S(1)}, u32[]{:S(2)}, u32[]{:S(2)}) collective-permute-start(f32[32,4,1,128]{3,0,2,1:T(8,128)S(1)} %get-tuple-element.192), channel_id=1, source_target_pairs={{0,4},{4,8},{8,12},{12,16},{16,20},{20,24},{24,28},{1,5},{5,9},{9,... | collective-permute-start | bytes 196616 | tf_op jit(solution)/shard_map/ppermute | solution.py:14
  566.4 9.9 %collective-permute-start.24 = (f32[32,4,10,1]{0,1,3,2:T(4,128)S(1)}, f32[32,4,10,1]{0,1,3,2:T(4,128)S(1)}, u32[]{:S(2)}, u32[]{:S(2)}) collective-permute-start(f32[32,4,10,1]{0,1,3,2:T(4,128)S(1)} %copy.274), channel_id=1, source_target_pairs={{1,0},{2,1},{3,2},{5,4},{6,5},{7,6},{9,8},{10,9},{11,10},{13,12},{... | collective-permute-start | bytes 15368 | tf_op jit(solution)/shard_map/ppermute | solution.py:17
  568.0 8.6 %collective-permute-start.25 = (f32[32,4,10,1]{0,1,3,2:T(4,128)S(1)}, f32[32,4,10,1]{0,1,3,2:T(4,128)S(1)}, u32[]{:S(2)}, u32[]{:S(2)}) collective-permute-start(f32[32,4,10,1]{0,1,3,2:T(4,128)S(1)} %copy.276), channel_id=1, source_target_pairs={{0,1},{1,2},{2,3},{4,5},{5,6},{6,7},{8,9},{9,10},{10,11},{12,13},{... | collective-permute-start | bytes 15368 | tf_op jit(solution)/shard_map/ppermute | solution.py:14
  578.5 49.0 %copy-start.32 = (f32[1,32,32]{1,2,0:T(8,128)S(1)}, f32[1,32,32]{1,2,0:T(8,128)}, u32[]{:S(2)}) copy-start(f32[1,32,32]{1,2,0:T(8,128)} %custom-call.23) | copy-start | bytes 12292
  634.0 5.0 collective-permute-start.26
  635.3 3.9 collective-permute-start.27
  640.8 10.0 %collective-permute-start.28 = (f32[32,4,10,1]{0,1,3,2:T(4,128)S(1)}, f32[32,4,10,1]{0,1,3,2:T(4,128)S(1)}, u32[]{:S(2)}, u32[]{:S(2)}) collective-permute-start(f32[32,4,10,1]{0,1,3,2:T(4,128)S(1)} %copy.287), channel_id=1, source_target_pairs={{1,0},{2,1},{3,2},{5,4},{6,5},{7,6},{9,8},{10,9},{11,10},{13,12},{... | collective-permute-start | bytes 15368 | tf_op jit(solution)/shard_map/ppermute | solution.py:17
  642.4 8.7 %collective-permute-start.29 = (f32[32,4,10,1]{0,1,3,2:T(4,128)S(1)}, f32[32,4,10,1]{0,1,3,2:T(4,128)S(1)}, u32[]{:S(2)}, u32[]{:S(2)}) collective-permute-start(f32[32,4,10,1]{0,1,3,2:T(4,128)S(1)} %copy.289), channel_id=1, source_target_pairs={{0,1},{1,2},{2,3},{4,5},{5,6},{6,7},{8,9},{9,10},{10,11},{12,13},{... | collective-permute-start | bytes 15368 | tf_op jit(solution)/shard_map/ppermute | solution.py:14
  653.7 53.9 %copy-start.31 = (f32[1,32,32]{1,2,0:T(8,128)S(1)}, f32[1,32,32]{1,2,0:T(8,128)}, u32[]{:S(2)}) copy-start(f32[1,32,32]{1,2,0:T(8,128)} %custom-call.25) | copy-start | bytes 12292
  654.9 58.1 %copy-start.6 = (f32[32,4,8,128]{3,0,2,1:T(8,128)S(1)}, f32[32,4,8,128]{3,0,2,1:T(8,128)}, u32[]{:S(2)}) copy-start(f32[32,4,8,128]{3,0,2,1:T(8,128)} %convolution_add_fusion.4) | copy-start | bytes 1572868
  708.6 5.0 collective-permute-start.30
  709.9 3.9 collective-permute-start.31
  714.5 7.1 collective-permute-start.32
  716.1 6.0 collective-permute-start.33
  (26 other events, 170.0 us)
